TPU v7x, 32 devices: a whole 2x2x4 slice. The times are simulated.
32 devices in a mesh: batch: 2 (over x), dap: 16 (over z, y, core).
Axes of the slice: x: 2, y: 2, z: 4, core: 2. Of those that a mesh axis runs over, the one named last changes fastest.
Arguments:
- pair_act: bfloat16 [512, 256, 128], P(('batch', 'dap')), parts along dimension 0
- pair_mask: int32 [512, 256], P(('batch', 'dap')), parts along dimension 0
- msa_act: bfloat16 [64, 512, 256], P(None, ('batch', 'dap')), parts along dimension 1
- opm_norm: bfloat16 [2, 2, 256], replicated
- opm_w_in: bfloat16 [2, 256, 2, 32], replicated
- opm_b_in: bfloat16 [2, 2, 32], replicated
- opm_w_out: bfloat16 [2, 1024, 128], replicated
- opm_b_out: bfloat16 [2, 128], replicated
- tri_norm_in: bfloat16 [2, 2, 128], replicated
- tri_w_ab: bfloat16 [2, 128, 4, 128], replicated
- tri_b_ab: bfloat16 [2, 4, 128], replicated
- tri_w_gate: bfloat16 [2, 128, 128], replicated
- tri_b_gate: bfloat16 [2, 128], replicated
- tri_norm_out: bfloat16 [2, 2, 128], replicated
- tri_w_out: bfloat16 [2, 128, 128], replicated
- tri_b_out: bfloat16 [2, 128], replicated
Outputs:
- output: bfloat16 [512, 256, 128], P(('batch', 'dap')), parts along dimension 0
There are 2 independent parts. A program takes and returns all parts, laid end to end along the dimension named above; an argument that names none is the same for every part.
All inputs are finite; a program needn't handle non-finite values.
Results may differ from a plain program's by a relative error of at most 0.0106302.
Values are sent between devices in bfloat16 or wider.
A program may use at most 1 GiB of HBM per device.

v0:
```python
import jax
import jax.numpy as jnp
from jax import lax
from jax.sharding import PartitionSpec as P
from jax.experimental import pallas as pl
from jax.experimental.pallas import tpu as pltpu

EPS = 1e-5
MESH = pl.DeviceIdType.MESH
F32, BF16 = jnp.float32, jnp.bfloat16
NL = 2
NT = 8
CC = 16
NZ = 4

NTD = (((1,), (1,)), ((), ()))


def place():
    me = lax.axis_index('dap')
    return me // 4, (me // 2) % 2, me % 2


def dap_of(z, y, c):
    return (z * 2 + y) * 2 + c


def sixteen(i):
    return pl.ds(pl.multiple_of(i * 16, 16), 16)


def kernel(zt_ref, mask_ref, al_ref, bown_ref, wq_ref, wab_ref, wg_ref, wo_ref, cols_ref, no_ref,
           out_ref,
           bg_ref, q_ref, wqt_ref, wabt_ref, wgt_ref, wot_ref, zn_ref, st_ref, aown_ref, arecv_ref, b_ref,
           obuf_ref, osend_ref, ost_ref, on_ref,
           sgi, rgi, sgd, rgd, sown, sa, ra, sz, rz, sd, rd, so, ro):
    z, y, c = place()
    chip = z * 2 + y
    ypart = dap_of(z, 1 - y, c)
    cpart = dap_of(z, y, 1 - c)

    bar = pltpu.get_barrier_semaphore()
    for r in range(1, 8):
        pl.semaphore_signal(bar, inc=1, device_id={'dap': lax.rem(chip + r, 8) * 2 + c}, device_id_type=MESH)
    pl.semaphore_signal(bar, inc=1, device_id={'dap': cpart}, device_id_type=MESH)
    pl.semaphore_wait(bar, 8)

    def bslot(l, ch, core):
        return bg_ref.at[l, :, sixteen((ch % 2 * 4 + ch // 2) * 2 + core), :]

    def g_ici(l, r):
        return pltpu.make_async_remote_copy(
            bown_ref.at[l], bslot(l, chip, c), sgi.at[l, r], rgi.at[l, r],
            device_id={'dap': lax.rem(chip + r, 8) * 2 + c}, device_id_type=MESH)

    def g_d2d(l, r):
        src = lax.rem(chip - r + 8, 8)
        return pltpu.make_async_remote_copy(
            bown_ref.at[l] if r == 0 else bslot(l, src, c), bslot(l, src, c), sgd.at[l, r], rgd.at[l, r],
            device_id={'dap': cpart}, device_id_type=MESH)

    def g_own(l):
        return pltpu.make_async_copy(bown_ref.at[l], bslot(l, chip, c), sown.at[l])

    def g_pass(l):
        for r in range(1, 8):
            g_ici(l, r).wait_recv()
            g_d2d(l, r).start()

    def g_finish(l):
        g_own(l).wait()
        for r in range(8):
            g_d2d(l, r).wait()
        for r in range(1, 8):
            g_ici(l, r).wait_send()

    def cp_a(l, t, kh):
        return pltpu.make_async_remote_copy(aown_ref.at[l, t, kh], arecv_ref.at[l, t, kh], sa.at[l, t, kh],
                                            ra.at[l, t, kh], device_id={'dap': ypart}, device_id_type=MESH)

    def cp_o(l, t):
        return pltpu.make_async_remote_copy(osend_ref.at[l, t], obuf_ref.at[l, y, t], so.at[l, t], ro.at[l, t],
                                            device_id={'dap': ypart}, device_id_type=MESH)

    def cp_d(l, zs, t, kh, core):
        blk = b_ref.at[l, zs, core, t, kh]
        return pltpu.make_async_remote_copy(blk, blk, sd.at[l, zs, t, kh], rd.at[l, zs, t, kh],
                                            device_id={'dap': cpart}, device_id_type=MESH)

    def cp_z(l, up, h, t, kh, zs, dev):
        blk = b_ref.at[l, zs, c, t, kh]
        return pltpu.make_async_remote_copy(blk, blk, sz.at[l, int(up), h, t, kh], rz.at[l, int(up), h, t, kh],
                                            device_id={'dap': dev}, device_id_type=MESH)

    def send_z(l, up, h, t, kh):
        zs, zd = (z - h, z + 1) if up else (z + h, z - 1)
        return cp_z(l, up, h, t, kh, zs, dap_of(zd, y, c))

    def can_send(up, h):
        return (z - h >= 0) & (z + 1 < NZ) if up else (z + h < NZ) & (z - 1 >= 0)

    def can_recv(up, h):
        return z - h - 1 >= 0 if up else z + h + 1 < NZ

    def arrive(l, h, t, kh):
        for up in (False, True):
            @pl.when(can_recv(up, h))
            def _():
                zs = z - h - 1 if up else z + h + 1
                cp_z(l, up, h, t, kh, zs, cpart).wait_recv()
                if h < NZ - 2:
                    @pl.when(can_send(up, h + 1))
                    def _():
                        send_z(l, up, h + 1, t, kh).start()
                cp_d(l, zs, t, kh, c).start()

    for l in range(NL):
        for r in range(1, 8):
            g_ici(l, r).start()
        g_d2d(l, 0).start()
        g_own(l).start()

    r_i = lax.broadcasted_iota(jnp.int32, (256, 256), 0)
    c_i = lax.broadcasted_iota(jnp.int32, (256, 256), 1)
    perm = ((r_i // 16 == c_i % 16) & (r_i % 16 == c_i // 16)).astype(F32).astype(BF16)

    def turn(w):
        return w.astype(F32).T.astype(BF16)

    def prepare(l):
        @pl.loop(0, 4)
        def _(blk):
            r2 = lax.broadcasted_iota(jnp.int32, (256, 1024), 0)
            k2 = lax.broadcasted_iota(jnp.int32, (256, 1024), 1)
            sel = ((k2 // 32 == r2 % 32) & (k2 % 32 == r2 // 32 + blk * 8)).astype(F32).astype(BF16)
            w = jnp.dot(sel, wq_ref[l], preferred_element_type=F32)
            wqt_ref[l, :, pl.ds(pl.multiple_of(blk * 256, 256), 256)] = w.T.astype(BF16)
        for qq in range(4):
            w = turn(wab_ref[l, :, qq * 128:(qq + 1) * 128])
            wabt_ref[l, :, qq * CC:(qq + 1) * CC, :] = w.reshape(NT, CC, 128)
        wgt_ref[l] = turn(wg_ref[l])
        wot_ref[l] = turn(wo_ref[l])

    def outer(l, kh):
        @pl.loop(0, 8)
        def _(dpp):
            half = pl.ds(kh * 128, 128)
            bt = jnp.concatenate([bg_ref[l, dpp * 2, half, :], bg_ref[l, dpp * 2 + 1, half, :]], axis=0)
            for par in range(2):
                for h in range(2):
                    rows = lax.dot_general(al_ref[l, pl.ds(par * 512 + h * 256, 256), :], bt, NTD,
                                           preferred_element_type=F32)
                    rows = (rows * (1.0 / 64)).astype(BF16).reshape(4, 2, 32, 256)
                    for e in range(2):
                        at = pl.ds(pl.multiple_of((dpp * 4 + e * 2 + par) * 32, 32), 32)
                        for i2 in range(2):
                            q_ref[pl.ds(h * 4, 4), at, i2 * 128:(i2 + 1) * 128] = rows[:, i2, :, e * 128:(e + 1) * 128]

        src = zt_ref if l == 0 else out_ref

        def rows(ip, _):
            upd = jnp.dot(wqt_ref[l], q_ref[ip], preferred_element_type=F32) + cols_ref[l, :, 0:1]
            zi = (src[kh, ip].astype(F32) + upd.astype(BF16).astype(F32)).astype(BF16)
            out_ref[kh, ip] = zi
            x = zi.astype(F32)
            xc = x - jnp.mean(x, axis=0, keepdims=True)
            var = jnp.mean(xc * xc, axis=0, keepdims=True)
            zn_ref[kh, ip] = (xc * lax.rsqrt(var + EPS) * cols_ref[l, :, 1:2] + cols_ref[l, :, 2:3]).astype(BF16)
            return 0

        lax.fori_loop(0, 8, rows, 0)

    def project(l, kh):
        def chunk(t, _):
            bias = jnp.concatenate([jnp.broadcast_to(cols_ref[l, sixteen(t), 5 + qq:6 + qq], (CC, 256))
                                    for qq in range(4)], axis=0)
            w = wabt_ref[l, t]

            def rows(ip, _):
                p = jnp.dot(w, zn_ref[kh, ip], preferred_element_type=F32) + bias
                m = mask_ref[kh, ip]
                at = (m * jax.nn.sigmoid(p[16:32]) * p[0:16]).astype(BF16)
                bt = (m * jax.nn.sigmoid(p[48:64]) * p[32:48]).astype(BF16)
                for i2 in range(2):
                    ln = slice(i2 * 128, (i2 + 1) * 128)
                    st_ref[sixteen(ip * 2 + i2), 0:128] = at[:, ln]
                    st_ref[sixteen(ip * 2 + i2), 128:256] = bt[:, ln]
                return 0

            lax.fori_loop(0, 8, rows, 0, unroll=4)
            ab = jnp.dot(perm, st_ref[...], preferred_element_type=F32).astype(BF16)
            aown_ref[l, t, kh] = ab[:, 0:128]
            b_ref[l, z, c, t, kh] = ab[:, 128:256]
            for up in (False, True):
                @pl.when(can_send(up, 0))
                def _():
                    send_z(l, up, 0, t, kh).start()
            cp_a(l, t, kh).start()
            cp_d(l, z, t, kh, c).start()
            return 0

        lax.fori_loop(0, NT, chunk, 0)

    def multiply(l, t):
        for kh in range(2):
            cp_a(l, t, kh).wait_recv()
            for zs in range(NZ):
                cp_d(l, zs, t, kh, 1 - c).wait_recv()
        for cc in range(CC):
            rs = pl.ds(cc * 16, 16)
            o = None
            lhs = jnp.concatenate([jnp.concatenate([r[l, t, kh, rs, :] for kh in range(2)], axis=1)
                                   for r in (aown_ref, arecv_ref)], axis=0)
            rhs = jnp.concatenate([jnp.concatenate([b_ref[l, zs, k, t, kh, rs, :] for kh in range(2)], axis=1)
                                   for zs in range(NZ) for k in range(2)], axis=0)
            o = lax.dot_general(lhs, rhs, NTD, preferred_element_type=F32)
            obuf_ref[l, y, t, rs, :] = o[0:16]
            osend_ref[l, t, rs, :] = o[16:32]
        cp_o(l, t).start()

    def drain(l):
        @pl.loop(0, NT)
        def _(t):
            cp_o(l, t).wait()
            for kh in range(2):
                cp_a(l, t, kh).wait_send()
                for zs in range(NZ):
                    cp_d(l, zs, t, kh, c).wait_send()
                for up in (False, True):
                    for h in range(NZ - 1):
                        @pl.when(can_send(up, h))
                        def _():
                            send_z(l, up, h, t, kh).wait_send()

    def finish(l):
        def load(t, cc, hh):
            return obuf_ref[l, hh, t, pl.ds(cc * 16, 16), :]

        zero = jnp.zeros((16, 128), F32)

        def add1(t, s):
            for cc in range(CC):
                s = tuple(s[hh] + load(t, cc, hh) for hh in range(2))
            return s

        tot = lax.fori_loop(0, NT, add1, (zero, zero))
        mean = tuple(s * (1.0 / 128) for s in tot)

        def add2(t, s):
            for cc in range(CC):
                d = tuple(load(t, cc, hh) - mean[hh] for hh in range(2))
                s = tuple(s[hh] + d[hh] * d[hh] for hh in range(2))
            return s

        sq = lax.fori_loop(0, NT, add2, (zero, zero))
        inv = tuple(lax.rsqrt(s * (1.0 / 128) + EPS) for s in sq)

        def norm(t, _):
            for cc in range(CC):
                for hh in range(2):
                    v = (load(t, cc, hh) - mean[hh]) * inv[hh] * no_ref[l, 0, t * CC + cc] + no_ref[l, 1, t * CC + cc]
                    ost_ref[pl.ds(cc * 16, 16), pl.ds(hh * 128, 128)] = v.astype(BF16)
            on = jnp.dot(perm, ost_ref[...], preferred_element_type=F32).astype(BF16).reshape(8, 2, CC, 256)
            for hh in range(2):
                for i2 in range(2):
                    on_ref[hh, :, sixteen(t), i2 * 128:(i2 + 1) * 128] = on[:, i2, :, hh * 128:(hh + 1) * 128]
            return 0

        lax.fori_loop(0, NT, norm, 0)

        for kh in range(2):
            def rows(ip, _):
                u = (jnp.dot(wot_ref[l], on_ref[kh, ip], preferred_element_type=F32) + cols_ref[l, :, 3:4]).astype(BF16)
                g = jax.nn.sigmoid(jnp.dot(wgt_ref[l], zn_ref[kh, ip], preferred_element_type=F32)
                                   + cols_ref[l, :, 4:5])
                out_ref[kh, ip] = (out_ref[kh, ip].astype(F32) + g * u.astype(F32)).astype(BF16)
                return 0

            lax.fori_loop(0, 8, rows, 0)

    prepare(0)
    g_pass(0)
    g_finish(0)
    for l in range(NL):
        for kh in range(2):
            outer(l, kh)
            project(l, kh)
        for h in range(NZ - 2):
            @pl.loop(0, 2 * NT)
            def _(n):
                arrive(l, h, n % NT, n // NT)
            if l == 0 and h == 0:
                g_pass(1)
                prepare(1)

        @pl.loop(0, NT)
        def _(t):
            arrive(l, NZ - 2, t, 0)

        @pl.loop(0, NT)
        def _(t):
            arrive(l, NZ - 2, t, 1)
            multiply(l, t)

        if l == 0:
            g_finish(1)
        drain(l)
        finish(l)


def solution(mesh):
    pair_spec = P(('batch', 'dap'), None, None)
    mask_spec = P(('batch', 'dap'), None)
    msa_spec = P(None, ('batch', 'dap'), None)
    vm = pl.BlockSpec(memory_space=pltpu.VMEM)
    dma = pltpu.SemaphoreType.DMA

    def bf(*shape):
        return pltpu.VMEM(shape, BF16)

    def f3(*shape):
        return pltpu.VMEM(shape, F32)

    call = pl.pallas_call(
        kernel,
        out_shape=jax.ShapeDtypeStruct((2, 8, 128, 256), BF16),
        in_specs=[vm] * 9 + [pl.BlockSpec(memory_space=pltpu.SMEM)],
        out_specs=vm,
        scratch_shapes=[
            bf(NL, 16, 256, 128), bf(8, 1024, 256),
            bf(NL, 128, 1024), bf(NL, NT, 4 * CC, 128), bf(NL, 128, 128), bf(NL, 128, 128),
            bf(2, 8, 128, 256), bf(256, 256),
            bf(NL, NT, 2, 256, 128), bf(NL, NT, 2, 256, 128), bf(NL, NZ, 2, NT, 2, 256, 128),
            f3(NL, 2, NT, 256, 128), f3(NL, NT, 256, 128), bf(256, 256), bf(2, 8, 128, 256),
            dma((NL, 8)), dma((NL, 8)), dma((NL, 8)), dma((NL, 8)), dma((NL,)),
            dma((NL, NT, 2)), dma((NL, NT, 2)),
            dma((NL, 2, NZ - 1, NT, 2)), dma((NL, 2, NZ - 1, NT, 2)),
            dma((NL, NZ, NT, 2)), dma((NL, NZ, NT, 2)),
            dma((NL, NT)), dma((NL, NT)),
        ],
        compiler_params=pltpu.CompilerParams(collective_id=0, has_side_effects=True),
        name='layers',
    )

    def device_fn(pair, mask, msa, opm_norm, opm_w_in, opm_b_in, opm_w_out, opm_b_out, tri_norm_in, tri_w_ab, tri_b_ab,
                  tri_w_gate, tri_b_gate, tri_norm_out, tri_w_out, tri_b_out):
        x = msa.astype(F32)
        xc = x - jnp.mean(x, axis=-1, keepdims=True)
        var = jnp.mean(xc * xc, axis=-1, keepdims=True)
        xh = xc * lax.rsqrt(var + EPS)
        nw = opm_norm.astype(F32)
        mn = (xh[None] * nw[:, 0][:, None, None] + nw[:, 1][:, None, None]).astype(BF16)
        bias = opm_b_in.astype(F32)
        b = (jnp.einsum('lmd,lsjm->ldjs', opm_w_in[:, :, 1], mn, preferred_element_type=F32)
             + bias[:, 1][:, :, None, None]).astype(BF16)
        b = b.reshape(2, 16, 2, 16, 64).transpose(0, 1, 3, 2, 4).reshape(2, 16, 16, 128)
        a = (jnp.einsum('lmc,lsim->lics', opm_w_in[:, :, 0], mn, preferred_element_type=F32)
             + bias[:, 0][:, None, :, None]).astype(BF16).reshape(2, 512, 64)
        al = jnp.concatenate([jnp.pad(a, ((0, 0), (0, 0), (0, 64))), jnp.pad(a, ((0, 0), (0, 0), (64, 0)))], axis=1)

        cols = jnp.concatenate([jnp.stack([opm_b_out, tri_norm_in[:, 0], tri_norm_in[:, 1], tri_b_out, tri_b_gate], axis=1),
                                tri_b_ab], axis=1).transpose(0, 2, 1).astype(F32)
        zt = pair.reshape(8, 2, 4, 2, 32, 128).transpose(3, 0, 5, 1, 2, 4).reshape(2, 8, 128, 256)
        mf = mask.reshape(8, 2, 4, 2, 32).transpose(3, 0, 1, 2, 4).reshape(2, 8, 1, 256).astype(F32)
        zt = call(zt, mf, al, b, opm_w_out, tri_w_ab.reshape(2, 128, 512), tri_w_gate, tri_w_out, cols,
                  tri_norm_out.astype(F32))
        return zt.reshape(2, 8, 128, 2, 4, 32).transpose(1, 3, 4, 0, 5, 2).reshape(16, 256, 128)

    return jax.shard_map(device_fn, mesh=mesh, in_specs=(pair_spec, mask_spec, msa_spec) + (P(),) * 13,
                         out_specs=pair_spec, check_vma=False)
```

profile of v0, /device:TPU:0, one launch (start us, length us, event | category | flops | bytes accessed | tf_op | source)
XLA Modules:
  0.0 229.9 jit_solution(9901032461559988445)
XLA Ops:
  0.0 0.0 copy-start
  0.0 0.0 copy-start.2
  0.0 1.3 convert_element_type.59.no_ref
  1.3 0.8 fusion.21
  2.1 0.8 fusion.20
  2.9 0.7 constant_dynamic-update-slice_fusion.4
  3.5 0.7 constant_dynamic-update-slice_fusion.3
  4.2 0.7 constant_dynamic-update-slice_fusion.2
  4.9 0.7 constant_dynamic-update-slice_fusion.1
  5.5 0.7 constant_dynamic-update-slice_fusion
  6.2 0.7 convert_element_type.45
  7.0 1.3 convert_reduce_fusion
  8.2 0.0 copy-done
  8.2 0.4 fusion.6
  8.6 0.1 convert_element_type.46
  8.8 0.7 convert_element_type.48.mask_ref
  9.5 0.8 copy.63
  10.2 0.0 copy-done.2
  10.2 0.0 copy-start.3
  10.2 0.8 reshape.62.wab_ref
  11.0 0.3 fusion.2
  11.4 0.0 copy-done.3
  11.4 0.4 fusion.4
  11.8 0.4 fusion.5
  12.3 0.5 copy.57
  12.7 0.6 copy.59
  13.3 0.0 copy-start.1
  13.3 0.2 copy.60
  13.5 0.8 reshape.61.bown_ref
  14.3 1.0 fusion.15.al_ref
  15.3 0.0 copy-done.1
  15.3 0.1 copy.54
  15.4 1.3 copy.64.zt_ref
  16.7 210.4 %layers.1 = bf16[2,8,128,256]{3,2,1,0:T(8,128)(2,1)} custom-call(bf16[2,8,128,256]{3,2,1,0:T(8,128)(2,1)} %copy.64.zt_ref, f32[2,8,1,256]{3,2,1,0:T(1,128)} %convert_element_type.48.mask_ref, bf16[2,1024,128]{2,1,0:T(8,128)(2,1)} %fusion.15.al_ref, bf16[2,16,16,128]{3,2,1,0:T(8,128)(2,1)} %reshape.61.bown_ref, bf16[2,1024,128]{2,1,0:T(8,128)(2,1)} %wq_ref.1, ...), custom_call_target="tpu_custom_call" | custom-call | tf_op jit(solution)/shard_map/layers/pallas_call | solution.py:365
  227.2 1.6 copy.65
  228.8 1.1 copy.66
  (4 shorter events, 0.0 us)
Async XLA Ops:
  0.0 8.2 %copy-start = (bf16[64,16,256]{2,1,0:T(8,128)(2,1)S(1)}, bf16[64,16,256]{2,1,0:T(8,128)(2,1)}, u32[]{:S(2)}) copy-start(bf16[64,16,256]{2,1,0:T(8,128)(2,1)} %param.18) | copy-start | bytes 1572868
  0.0 10.2 %copy-start.2 = (bf16[2,128,4,128]{3,2,1,0:T(4,128)(2,1)S(1)}, bf16[2,128,4,128]{3,2,1,0:T(4,128)(2,1)}, u32[]{:S(2)}) copy-start(bf16[2,128,4,128]{3,2,1,0:T(4,128)(2,1)} %param.25) | copy-start | bytes 786436
  10.2 1.1 copy-start.3
  13.3 2.0 copy-start.1
where the time goes:
time: 230 us
  Pallas kernels  210 us (91%)
  local copies, waits for them, and re-layouts  13.5 us (6%)
  other arithmetic  4.98 us (2%)
    pallas_call x1, Pallas kernels, device_fn(): call(zt, mf, al, b, opm_w_out, tri_w_ab.reshape(2, 128, 512), tri_w_gate,...  210 us

commit v1 on v0

--- a/solution.py
+++ b/solution.py
@@ -11,6 +11,8 @@
 NL = 2
 NT = 8
 CC = 16
+TG = 2
+NG = NT // TG
 NZ = 4
 
 NTD = (((1,), (1,)), ((), ()))
@@ -29,9 +31,10 @@
     return pl.ds(pl.multiple_of(i * 16, 16), 16)
 
 
-def kernel(zt_ref, mask_ref, al_ref, bown_ref, wq_ref, wab_ref, wg_ref, wo_ref, cols_ref, no_ref,
+def kernel(zt_ref, maskin_ref, al_ref, bown_ref, wq_ref, wab_ref, wg_ref, wo_ref,
+           bq_ref, ni_ref, bo_ref, bgate_ref, bab_ref, nout_ref,
            out_ref,
-           bg_ref, q_ref, wqt_ref, wabt_ref, wgt_ref, wot_ref, zn_ref, st_ref, aown_ref, arecv_ref, b_ref,
+           cols_ref, no_ref, mask_ref, bg_ref, q_ref, wqt_ref, wabt_ref, wgt_ref, wot_ref, zn_ref, st_ref, aown_ref, arecv_ref, b_ref,
            obuf_ref, osend_ref, ost_ref, on_ref,
            sgi, rgi, sgd, rgd, sown, sa, ra, sz, rz, sd, rd, so, ro):
     z, y, c = place()
@@ -74,27 +77,30 @@
         for r in range(1, 8):
             g_ici(l, r).wait_send()
 
-    def cp_a(l, t, kh):
-        return pltpu.make_async_remote_copy(aown_ref.at[l, t, kh], arecv_ref.at[l, t, kh], sa.at[l, t, kh],
-                                            ra.at[l, t, kh], device_id={'dap': ypart}, device_id_type=MESH)
+    def grp(g):
+        return pl.ds(g * TG, TG)
+
+    def cp_a(l, g, kh):
+        return pltpu.make_async_remote_copy(aown_ref.at[l, kh, grp(g)], arecv_ref.at[l, kh, grp(g)], sa.at[l, g, kh],
+                                            ra.at[l, g, kh], device_id={'dap': ypart}, device_id_type=MESH)
 
     def cp_o(l, t):
         return pltpu.make_async_remote_copy(osend_ref.at[l, t], obuf_ref.at[l, y, t], so.at[l, t], ro.at[l, t],
                                             device_id={'dap': ypart}, device_id_type=MESH)
 
-    def cp_d(l, zs, t, kh, core):
-        blk = b_ref.at[l, zs, core, t, kh]
-        return pltpu.make_async_remote_copy(blk, blk, sd.at[l, zs, t, kh], rd.at[l, zs, t, kh],
+    def cp_d(l, zs, g, kh, core):
+        blk = b_ref.at[l, zs, core, kh, grp(g)]
+        return pltpu.make_async_remote_copy(blk, blk, sd.at[l, zs, g, kh], rd.at[l, zs, g, kh],
                                             device_id={'dap': cpart}, device_id_type=MESH)
 
-    def cp_z(l, up, h, t, kh, zs, dev):
-        blk = b_ref.at[l, zs, c, t, kh]
-        return pltpu.make_async_remote_copy(blk, blk, sz.at[l, int(up), h, t, kh], rz.at[l, int(up), h, t, kh],
+    def cp_z(l, up, h, g, kh, zs, dev):
+        blk = b_ref.at[l, zs, c, kh, grp(g)]
+        return pltpu.make_async_remote_copy(blk, blk, sz.at[l, int(up), h, g, kh], rz.at[l, int(up), h, g, kh],
                                             device_id={'dap': dev}, device_id_type=MESH)
 
-    def send_z(l, up, h, t, kh):
+    def send_z(l, up, h, g, kh):
         zs, zd = (z - h, z + 1) if up else (z + h, z - 1)
-        return cp_z(l, up, h, t, kh, zs, dap_of(zd, y, c))
+        return cp_z(l, up, h, g, kh, zs, dap_of(zd, y, c))
 
     def can_send(up, h):
         return (z - h >= 0) & (z + 1 < NZ) if up else (z + h < NZ) & (z - 1 >= 0)
@@ -102,24 +108,26 @@
     def can_recv(up, h):
         return z - h - 1 >= 0 if up else z + h + 1 < NZ
 
-    def arrive(l, h, t, kh):
+    def arrive(l, h, g, kh):
         for up in (False, True):
             @pl.when(can_recv(up, h))
             def _():
                 zs = z - h - 1 if up else z + h + 1
-                cp_z(l, up, h, t, kh, zs, cpart).wait_recv()
+                cp_z(l, up, h, g, kh, zs, cpart).wait_recv()
                 if h < NZ - 2:
                     @pl.when(can_send(up, h + 1))
                     def _():
-                        send_z(l, up, h + 1, t, kh).start()
-                cp_d(l, zs, t, kh, c).start()
-
-    for l in range(NL):
+                        send_z(l, up, h + 1, g, kh).start()
+                cp_d(l, zs, g, kh, c).start()
+
+    def g_start(l):
         for r in range(1, 8):
             g_ici(l, r).start()
         g_d2d(l, 0).start()
         g_own(l).start()
 
+    g_start(0)
+
     r_i = lax.broadcasted_iota(jnp.int32, (256, 256), 0)
     c_i = lax.broadcasted_iota(jnp.int32, (256, 256), 1)
     perm = ((r_i // 16 == c_i % 16) & (r_i % 16 == c_i // 16)).astype(F32).astype(BF16)
@@ -128,6 +136,13 @@
         return w.astype(F32).T.astype(BF16)
 
     def prepare(l):
+        rows = [bq_ref[l:l + 1, :], ni_ref[l, 0:1, :], ni_ref[l, 1:2, :], bo_ref[l:l + 1, :], bgate_ref[l:l + 1, :]]
+        rows = rows + [bab_ref[l, qq:qq + 1, :] for qq in range(4)]
+        rows = [v.astype(F32) for v in rows] + [jnp.zeros((7, 128), F32)]
+        cols_ref[l] = jnp.concatenate(rows, axis=0).T
+        for n in range(2):
+            no_ref[l, n] = jnp.broadcast_to(nout_ref[l, n:n + 1, :].astype(F32), (128, 128)).T
+
         @pl.loop(0, 4)
         def _(blk):
             r2 = lax.broadcasted_iota(jnp.int32, (256, 1024), 0)
@@ -189,29 +204,32 @@
 
             lax.fori_loop(0, 8, rows, 0, unroll=4)
             ab = jnp.dot(perm, st_ref[...], preferred_element_type=F32).astype(BF16)
-            aown_ref[l, t, kh] = ab[:, 0:128]
-            b_ref[l, z, c, t, kh] = ab[:, 128:256]
+            aown_ref[l, kh, t] = ab[:, 0:128]
+            b_ref[l, z, c, kh, t] = ab[:, 128:256]
+            return 0
+
+        @pl.loop(0, NG)
+        def _(g):
+            lax.fori_loop(g * TG, g * TG + TG, chunk, 0)
             for up in (False, True):
                 @pl.when(can_send(up, 0))
                 def _():
-                    send_z(l, up, 0, t, kh).start()
-            cp_a(l, t, kh).start()
-            cp_d(l, z, t, kh, c).start()
-            return 0
-
-        lax.fori_loop(0, NT, chunk, 0)
+                    send_z(l, up, 0, g, kh).start()
+            cp_a(l, g, kh).start()
+            cp_d(l, z, g, kh, c).start()
+
+    def ready(l, g):
+        for kh in range(2):
+            cp_a(l, g, kh).wait_recv()
+            for zs in range(NZ):
+                cp_d(l, zs, g, kh, 1 - c).wait_recv()
 
     def multiply(l, t):
-        for kh in range(2):
-            cp_a(l, t, kh).wait_recv()
-            for zs in range(NZ):
-                cp_d(l, zs, t, kh, 1 - c).wait_recv()
         for cc in range(CC):
             rs = pl.ds(cc * 16, 16)
-            o = None
-            lhs = jnp.concatenate([jnp.concatenate([r[l, t, kh, rs, :] for kh in range(2)], axis=1)
+            lhs = jnp.concatenate([jnp.concatenate([r[l, kh, t, rs, :] for kh in range(2)], axis=1)
                                    for r in (aown_ref, arecv_ref)], axis=0)
-            rhs = jnp.concatenate([jnp.concatenate([b_ref[l, zs, k, t, kh, rs, :] for kh in range(2)], axis=1)
+            rhs = jnp.concatenate([jnp.concatenate([b_ref[l, zs, k, kh, t, rs, :] for kh in range(2)], axis=1)
                                    for zs in range(NZ) for k in range(2)], axis=0)
             o = lax.dot_general(lhs, rhs, NTD, preferred_element_type=F32)
             obuf_ref[l, y, t, rs, :] = o[0:16]
@@ -222,15 +240,18 @@
         @pl.loop(0, NT)
         def _(t):
             cp_o(l, t).wait()
+
+        @pl.loop(0, NG)
+        def _(g):
             for kh in range(2):
-                cp_a(l, t, kh).wait_send()
+                cp_a(l, g, kh).wait_send()
                 for zs in range(NZ):
-                    cp_d(l, zs, t, kh, c).wait_send()
+                    cp_d(l, zs, g, kh, c).wait_send()
                 for up in (False, True):
                     for h in range(NZ - 1):
                         @pl.when(can_send(up, h))
                         def _():
-                            send_z(l, up, h, t, kh).wait_send()
+                            send_z(l, up, h, g, kh).wait_send()
 
     def finish(l):
         def load(t, cc, hh):
@@ -258,7 +279,8 @@
         def norm(t, _):
             for cc in range(CC):
                 for hh in range(2):
-                    v = (load(t, cc, hh) - mean[hh]) * inv[hh] * no_ref[l, 0, t * CC + cc] + no_ref[l, 1, t * CC + cc]
+                    one = pl.ds(t * CC + cc, 1)
+                    v = (load(t, cc, hh) - mean[hh]) * inv[hh] * no_ref[l, 0, one, :] + no_ref[l, 1, one, :]
                     ost_ref[pl.ds(cc * 16, 16), pl.ds(hh * 128, 128)] = v.astype(BF16)
             on = jnp.dot(perm, ost_ref[...], preferred_element_type=F32).astype(BF16).reshape(8, 2, CC, 256)
             for hh in range(2):
@@ -279,6 +301,11 @@
             lax.fori_loop(0, 8, rows, 0)
 
     prepare(0)
+    m = maskin_ref[...].astype(F32)
+    for kh in range(2):
+        half = jnp.concatenate([m[:, zz * 64 + kh * 32:zz * 64 + kh * 32 + 32] for zz in range(NZ)], axis=1)
+        for i in range(16):
+            mask_ref[kh, i // 2, :, i % 2 * 128:(i % 2 + 1) * 128] = half[i:i + 1, :]
     g_pass(0)
     g_finish(0)
     for l in range(NL):
@@ -286,26 +313,33 @@
             outer(l, kh)
             project(l, kh)
         for h in range(NZ - 2):
-            @pl.loop(0, 2 * NT)
+            @pl.loop(0, 2 * NG)
             def _(n):
-                arrive(l, h, n % NT, n // NT)
+                arrive(l, h, n % NG, n // NG)
             if l == 0 and h == 0:
-                g_pass(1)
                 prepare(1)
-
-        @pl.loop(0, NT)
-        def _(t):
-            arrive(l, NZ - 2, t, 0)
-
-        @pl.loop(0, NT)
-        def _(t):
-            arrive(l, NZ - 2, t, 1)
-            multiply(l, t)
-
+        if l == 0:
+            g_start(1)
+
+        @pl.loop(0, NG)
+        def _(g):
+            arrive(l, NZ - 2, g, 0)
+
+        @pl.loop(0, NG)
+        def _(g):
+            arrive(l, NZ - 2, g, 1)
+            ready(l, g)
+
+            @pl.loop(0, TG)
+            def _(k):
+                multiply(l, g * TG + k)
+
+        if l == 0:
+            g_pass(1)
+        drain(l)
+        finish(l)
         if l == 0:
             g_finish(1)
-        drain(l)
-        finish(l)
 
 
 def solution(mesh):
@@ -324,18 +358,19 @@
     call = pl.pallas_call(
         kernel,
         out_shape=jax.ShapeDtypeStruct((2, 8, 128, 256), BF16),
-        in_specs=[vm] * 9 + [pl.BlockSpec(memory_space=pltpu.SMEM)],
+        in_specs=[vm] * 14,
         out_specs=vm,
         scratch_shapes=[
+            f3(NL, 128, 16), f3(NL, 2, 128, 128), f3(2, 8, 1, 256),
             bf(NL, 16, 256, 128), bf(8, 1024, 256),
             bf(NL, 128, 1024), bf(NL, NT, 4 * CC, 128), bf(NL, 128, 128), bf(NL, 128, 128),
             bf(2, 8, 128, 256), bf(256, 256),
-            bf(NL, NT, 2, 256, 128), bf(NL, NT, 2, 256, 128), bf(NL, NZ, 2, NT, 2, 256, 128),
+            bf(NL, 2, NT, 256, 128), bf(NL, 2, NT, 256, 128), bf(NL, NZ, 2, 2, NT, 256, 128),
             f3(NL, 2, NT, 256, 128), f3(NL, NT, 256, 128), bf(256, 256), bf(2, 8, 128, 256),
             dma((NL, 8)), dma((NL, 8)), dma((NL, 8)), dma((NL, 8)), dma((NL,)),
-            dma((NL, NT, 2)), dma((NL, NT, 2)),
-            dma((NL, 2, NZ - 1, NT, 2)), dma((NL, 2, NZ - 1, NT, 2)),
-            dma((NL, NZ, NT, 2)), dma((NL, NZ, NT, 2)),
+            dma((NL, NG, 2)), dma((NL, NG, 2)),
+            dma((NL, 2, NZ - 1, NG, 2)), dma((NL, 2, NZ - 1, NG, 2)),
+            dma((NL, NZ, NG, 2)), dma((NL, NZ, NG, 2)),
             dma((NL, NT)), dma((NL, NT)),
         ],
         compiler_params=pltpu.CompilerParams(collective_id=0, has_side_effects=True),
@@ -358,12 +393,9 @@
              + bias[:, 0][:, None, :, None]).astype(BF16).reshape(2, 512, 64)
         al = jnp.concatenate([jnp.pad(a, ((0, 0), (0, 0), (0, 64))), jnp.pad(a, ((0, 0), (0, 0), (64, 0)))], axis=1)
 
-        cols = jnp.concatenate([jnp.stack([opm_b_out, tri_norm_in[:, 0], tri_norm_in[:, 1], tri_b_out, tri_b_gate], axis=1),
-                                tri_b_ab], axis=1).transpose(0, 2, 1).astype(F32)
         zt = pair.reshape(8, 2, 4, 2, 32, 128).transpose(3, 0, 5, 1, 2, 4).reshape(2, 8, 128, 256)
-        mf = mask.reshape(8, 2, 4, 2, 32).transpose(3, 0, 1, 2, 4).reshape(2, 8, 1, 256).astype(F32)
-        zt = call(zt, mf, al, b, opm_w_out, tri_w_ab.reshape(2, 128, 512), tri_w_gate, tri_w_out, cols,
-                  tri_norm_out.astype(F32))
+        zt = call(zt, mask, al, b, opm_w_out, tri_w_ab.reshape(2, 128, 512), tri_w_gate, tri_w_out,
+                  opm_b_out, tri_norm_in, tri_b_out, tri_b_gate, tri_b_ab, tri_norm_out)
         return zt.reshape(2, 8, 128, 2, 4, 32).transpose(1, 3, 4, 0, 5, 2).reshape(16, 256, 128)
 
     return jax.shard_map(device_fn, mesh=mesh, in_specs=(pair_spec, mask_spec, msa_spec) + (P(),) * 13,

time: 230 us -> 224 us (0.974)
  local copies, waits for them, and re-layouts: 13.5 us -> 8.57 us
    unnamed x13 -> x9, local copies, waits for them, and re-layouts: 2.69 us -> 0.03 us
where the time goes in v1:
time: 224 us; the launch traced here: 223 us
  Pallas kernels  210 us (94%)
  local copies, waits for them, and re-layouts  8.57 us (4%)
  other arithmetic  3.97 us (2%)
    pallas_call x1, Pallas kernels, device_fn(): call(zt, mask, al, b, opm_w_out, tri_w_ab.reshape(2, 128, 512), tri_w_gat...  210 us

profile of v1, /device:TPU:0, one launch (start us, length us, event | category | flops | bytes accessed | tf_op | source)
XLA Modules:
  0.0 223.3 jit_solution(12770141218249946231)
XLA Ops:
  0.0 0.0 copy-start
  0.0 0.0 copy-start.2
  0.0 0.8 fusion.21
  0.8 0.8 fusion.20
  1.5 1.3 convert_reduce_fusion
  2.8 1.4 fusion.6
  4.2 0.0 copy-done.2
  4.3 0.0 copy-start.3
  4.3 0.8 reshape.46.wab_ref
  5.1 0.0 copy-done
  5.1 0.3 fusion.2
  5.4 0.0 copy-done.3
  5.4 0.4 fusion.4
  5.9 0.4 fusion.5
  6.3 0.5 copy.32
  6.7 0.6 copy.34
  7.3 0.0 copy-start.1
  7.3 0.2 copy.35
  7.6 0.8 reshape.45.bown_ref
  8.4 1.0 fusion.15.al_ref
  9.3 0.0 copy-done.1
  9.3 0.1 copy.30
  9.5 1.3 copy.36.zt_ref
  10.8 209.8 %layers.1 = bf16[2,8,128,256]{3,2,1,0:T(8,128)(2,1)} custom-call(bf16[2,8,128,256]{3,2,1,0:T(8,128)(2,1)} %copy.36.zt_ref, s32[16,256]{1,0:T(8,128)} %maskin_ref.1, bf16[2,1024,128]{2,1,0:T(8,128)(2,1)} %fusion.15.al_ref, bf16[2,16,16,128]{3,2,1,0:T(8,128)(2,1)} %reshape.45.bown_ref, bf16[2,1024,128]{2,1,0:T(8,128)(2,1)} %wq_ref.1, ...), custom_call_target="tpu_custom_call" | custom-call | tf_op jit(solution)/shard_map/layers/pallas_call | solution.py:397
  220.5 1.6 copy.37
  222.2 1.1 copy.38
  (3 shorter events, 0.0 us)
Async XLA Ops:
  0.0 5.1 %copy-start = (bf16[64,16,256]{2,1,0:T(8,128)(2,1)S(1)}, bf16[64,16,256]{2,1,0:T(8,128)(2,1)}, u32[]{:S(2)}) copy-start(bf16[64,16,256]{2,1,0:T(8,128)(2,1)} %param.18) | copy-start | bytes 1572868
  0.0 4.2 %copy-start.2 = (bf16[2,128,4,128]{3,2,1,0:T(4,128)(2,1)S(1)}, bf16[2,128,4,128]{3,2,1,0:T(4,128)(2,1)}, u32[]{:S(2)}) copy-start(bf16[2,128,4,128]{3,2,1,0:T(4,128)(2,1)} %param.25) | copy-start | bytes 786436
  4.3 1.2 copy-start.3
  7.3 2.0 copy-start.1

commit v2 on v1

--- a/solution.py
+++ b/solution.py
@@ -11,7 +11,7 @@
 NL = 2
 NT = 8
 CC = 16
-TG = 2
+TG = 1
 NG = NT // TG
 NZ = 4
 
@@ -114,11 +114,14 @@
             def _():
                 zs = z - h - 1 if up else z + h + 1
                 cp_z(l, up, h, g, kh, zs, cpart).wait_recv()
-                if h < NZ - 2:
-                    @pl.when(can_send(up, h + 1))
-                    def _():
-                        send_z(l, up, h + 1, g, kh).start()
                 cp_d(l, zs, g, kh, c).start()
+
+    def forward(l, h, g):
+        for up in (False, True):
+            @pl.when(can_send(up, h + 1))
+            def _():
+                for kh in range(2):
+                    send_z(l, up, h + 1, g, kh).start()
 
     def g_start(l):
         for r in range(1, 8):
@@ -312,22 +315,31 @@
         for kh in range(2):
             outer(l, kh)
             project(l, kh)
-        for h in range(NZ - 2):
-            @pl.loop(0, 2 * NG)
-            def _(n):
-                arrive(l, h, n % NG, n // NG)
-            if l == 0 and h == 0:
-                prepare(1)
+        @pl.loop(0, NG)
+        def _(g):
+            arrive(l, 0, g, 0)
+
+        @pl.loop(0, NG)
+        def _(g):
+            arrive(l, 0, g, 1)
+            forward(l, 0, g)
+
+        if l == 0:
+            prepare(1)
+
+        @pl.loop(0, NG)
+        def _(g):
+            for kh in range(2):
+                arrive(l, 1, g, kh)
+            forward(l, 1, g)
+
         if l == 0:
             g_start(1)
 
         @pl.loop(0, NG)
         def _(g):
-            arrive(l, NZ - 2, g, 0)
-
-        @pl.loop(0, NG)
-        def _(g):
-            arrive(l, NZ - 2, g, 1)
+            for kh in range(2):
+                arrive(l, 2, g, kh)
             ready(l, g)
 
             @pl.loop(0, TG)

time: 224 us -> 215 us (0.960)
  Pallas kernels: 210 us -> 201 us
    pallas_call x1, Pallas kernels: 210 us -> 201 us  [device_fn(): call(zt, mask, al, b, opm_w_out, tri_w_ab.reshape(2, 128, 512), tri_w_gat...]
where the time goes in v2:
time: 215 us
  Pallas kernels  201 us (93%)
  local copies, waits for them, and re-layouts  8.57 us (4%)
  other arithmetic  3.97 us (2%)
    pallas_call x1, Pallas kernels, device_fn(): call(zt, mask, al, b, opm_w_out, tri_w_ab.reshape(2, 128, 512), tri_w_gat...  201 us

profile of v2, /device:TPU:0, one launch (start us, length us, event | category | flops | bytes accessed | tf_op | source)
XLA Modules:
  0.0 214.9 jit_solution(7166132986095084147)
XLA Ops:
  0.0 0.0 copy-start
  0.0 0.0 copy-start.2
  0.0 0.8 fusion.21
  0.8 0.8 fusion.20
  1.5 1.3 convert_reduce_fusion
  2.8 1.4 fusion.6
  4.2 0.0 copy-done.2
  4.3 0.0 copy-start.3
  4.3 0.8 reshape.46.wab_ref
  5.1 0.0 copy-done
  5.1 0.3 fusion.2
  5.4 0.0 copy-done.3
  5.4 0.4 fusion.4
  5.9 0.4 fusion.5
  6.3 0.5 copy.32
  6.7 0.6 copy.34
  7.3 0.0 copy-start.1
  7.3 0.2 copy.35
  7.6 0.8 reshape.45.bown_ref
  8.4 1.0 fusion.15.al_ref
  9.3 0.0 copy-done.1
  9.3 0.1 copy.30
  9.5 1.3 copy.36.zt_ref
  10.8 201.4 %layers.1 = bf16[2,8,128,256]{3,2,1,0:T(8,128)(2,1)} custom-call(bf16[2,8,128,256]{3,2,1,0:T(8,128)(2,1)} %copy.36.zt_ref, s32[16,256]{1,0:T(8,128)} %maskin_ref.1, bf16[2,1024,128]{2,1,0:T(8,128)(2,1)} %fusion.15.al_ref, bf16[2,16,16,128]{3,2,1,0:T(8,128)(2,1)} %reshape.45.bown_ref, bf16[2,1024,128]{2,1,0:T(8,128)(2,1)} %wq_ref.1, ...), custom_call_target="tpu_custom_call" | custom-call | tf_op jit(solution)/shard_map/layers/pallas_call | solution.py:409
  212.2 1.6 copy.37
  213.8 1.1 copy.38
  (3 shorter events, 0.0 us)
Async XLA Ops:
  0.0 5.1 %copy-start = (bf16[64,16,256]{2,1,0:T(8,128)(2,1)S(1)}, bf16[64,16,256]{2,1,0:T(8,128)(2,1)}, u32[]{:S(2)}) copy-start(bf16[64,16,256]{2,1,0:T(8,128)(2,1)} %param.18) | copy-start | bytes 1572868
  0.0 4.2 %copy-start.2 = (bf16[2,128,4,128]{3,2,1,0:T(4,128)(2,1)S(1)}, bf16[2,128,4,128]{3,2,1,0:T(4,128)(2,1)}, u32[]{:S(2)}) copy-start(bf16[2,128,4,128]{3,2,1,0:T(4,128)(2,1)} %param.25) | copy-start | bytes 786436
  4.3 1.2 copy-start.3
  7.3 2.0 copy-start.1

commit v3 on v2

--- a/solution.py
+++ b/solution.py
@@ -38,44 +38,59 @@
            obuf_ref, osend_ref, ost_ref, on_ref,
            sgi, rgi, sgd, rgd, sown, sa, ra, sz, rz, sd, rd, so, ro):
     z, y, c = place()
-    chip = z * 2 + y
     ypart = dap_of(z, 1 - y, c)
     cpart = dap_of(z, y, 1 - c)
 
     bar = pltpu.get_barrier_semaphore()
-    for r in range(1, 8):
-        pl.semaphore_signal(bar, inc=1, device_id={'dap': lax.rem(chip + r, 8) * 2 + c}, device_id_type=MESH)
+    for r in range(1, NZ):
+        pl.semaphore_signal(bar, inc=1, device_id={'dap': dap_of(lax.rem(z + r, NZ), y, c)}, device_id_type=MESH)
+    pl.semaphore_signal(bar, inc=1, device_id={'dap': ypart}, device_id_type=MESH)
     pl.semaphore_signal(bar, inc=1, device_id={'dap': cpart}, device_id_type=MESH)
-    pl.semaphore_wait(bar, 8)
-
-    def bslot(l, ch, core):
-        return bg_ref.at[l, :, sixteen((ch % 2 * 4 + ch // 2) * 2 + core), :]
-
-    def g_ici(l, r):
+    pl.semaphore_wait(bar, NZ + 1)
+
+    def bslot(l, zz, yy, core):
+        return bg_ref.at[l, :, sixteen((yy * NZ + zz) * 2 + core), :]
+
+    def g_z(l, r):
         return pltpu.make_async_remote_copy(
-            bown_ref.at[l], bslot(l, chip, c), sgi.at[l, r], rgi.at[l, r],
-            device_id={'dap': lax.rem(chip + r, 8) * 2 + c}, device_id_type=MESH)
-
-    def g_d2d(l, r):
-        src = lax.rem(chip - r + 8, 8)
-        return pltpu.make_async_remote_copy(
-            bown_ref.at[l] if r == 0 else bslot(l, src, c), bslot(l, src, c), sgd.at[l, r], rgd.at[l, r],
-            device_id={'dap': cpart}, device_id_type=MESH)
+            bown_ref.at[l], bslot(l, z, y, c), sgi.at[l, r], rgi.at[l, r],
+            device_id={'dap': dap_of(lax.rem(z + r, NZ), y, c)}, device_id_type=MESH)
+
+    def g_fwd(l, r, other):
+        zs = lax.rem(z - r + NZ, NZ)
+        src = bown_ref.at[l] if r == 0 else bslot(l, zs, y, c)
+        if other == 0:
+            return pltpu.make_async_remote_copy(src, bslot(l, zs, y, c), sgi.at[l, NZ + r], rgi.at[l, NZ + r],
+                                                device_id={'dap': ypart}, device_id_type=MESH)
+        if other == 1:
+            return pltpu.make_async_remote_copy(src, bslot(l, zs, y, c), sgd.at[l, r], rgd.at[l, r],
+                                                device_id={'dap': cpart}, device_id_type=MESH)
+        far = bslot(l, zs, 1 - y, c)
+        return pltpu.make_async_remote_copy(far, far, sgd.at[l, NZ + r], rgd.at[l, NZ + r],
+                                            device_id={'dap': cpart}, device_id_type=MESH)
 
     def g_own(l):
-        return pltpu.make_async_copy(bown_ref.at[l], bslot(l, chip, c), sown.at[l])
-
-    def g_pass(l):
-        for r in range(1, 8):
-            g_ici(l, r).wait_recv()
-            g_d2d(l, r).start()
+        return pltpu.make_async_copy(bown_ref.at[l], bslot(l, z, y, c), sown.at[l])
+
+    def g_pass_z(l):
+        for r in range(1, NZ):
+            g_z(l, r).wait_recv()
+            g_fwd(l, r, 0).start()
+            g_fwd(l, r, 1).start()
+
+    def g_pass_y(l):
+        for r in range(NZ):
+            g_fwd(l, r, 0).wait_recv()
+            g_fwd(l, r, 2).start()
 
     def g_finish(l):
         g_own(l).wait()
-        for r in range(8):
-            g_d2d(l, r).wait()
-        for r in range(1, 8):
-            g_ici(l, r).wait_send()
+        for r in range(NZ):
+            g_fwd(l, r, 1).wait()
+            g_fwd(l, r, 2).wait()
+            g_fwd(l, r, 0).wait_send()
+            if r > 0:
+                g_z(l, r).wait_send()
 
     def grp(g):
         return pl.ds(g * TG, TG)
@@ -124,12 +139,14 @@
                     send_z(l, up, h + 1, g, kh).start()
 
     def g_start(l):
-        for r in range(1, 8):
-            g_ici(l, r).start()
-        g_d2d(l, 0).start()
+        for r in range(1, NZ):
+            g_z(l, r).start()
         g_own(l).start()
 
     g_start(0)
+    g_fwd(0, 0, 0).start()
+    g_fwd(0, 0, 1).start()
+    g_start(1)
 
     r_i = lax.broadcasted_iota(jnp.int32, (256, 256), 0)
     c_i = lax.broadcasted_iota(jnp.int32, (256, 256), 1)
@@ -160,7 +177,7 @@
         wot_ref[l] = turn(wo_ref[l])
 
     def outer(l, kh):
-        @pl.loop(0, 8)
+        @pl.loop(0, 8, unroll=8)
         def _(dpp):
             half = pl.ds(kh * 128, 128)
             bt = jnp.concatenate([bg_ref[l, dpp * 2, half, :], bg_ref[l, dpp * 2 + 1, half, :]], axis=0)
@@ -186,7 +203,7 @@
             zn_ref[kh, ip] = (xc * lax.rsqrt(var + EPS) * cols_ref[l, :, 1:2] + cols_ref[l, :, 2:3]).astype(BF16)
             return 0
 
-        lax.fori_loop(0, 8, rows, 0)
+        lax.fori_loop(0, 8, rows, 0, unroll=8)
 
     def project(l, kh):
         def chunk(t, _):
@@ -205,7 +222,7 @@
                     st_ref[sixteen(ip * 2 + i2), 128:256] = bt[:, ln]
                 return 0
 
-            lax.fori_loop(0, 8, rows, 0, unroll=4)
+            lax.fori_loop(0, 8, rows, 0, unroll=8)
             ab = jnp.dot(perm, st_ref[...], preferred_element_type=F32).astype(BF16)
             aown_ref[l, kh, t] = ab[:, 0:128]
             b_ref[l, z, c, kh, t] = ab[:, 128:256]
@@ -267,7 +284,7 @@
                 s = tuple(s[hh] + load(t, cc, hh) for hh in range(2))
             return s
 
-        tot = lax.fori_loop(0, NT, add1, (zero, zero))
+        tot = lax.fori_loop(0, NT, add1, (zero, zero), unroll=2)
         mean = tuple(s * (1.0 / 128) for s in tot)
 
         def add2(t, s):
@@ -276,7 +293,7 @@
                 s = tuple(s[hh] + d[hh] * d[hh] for hh in range(2))
             return s
 
-        sq = lax.fori_loop(0, NT, add2, (zero, zero))
+        sq = lax.fori_loop(0, NT, add2, (zero, zero), unroll=2)
         inv = tuple(lax.rsqrt(s * (1.0 / 128) + EPS) for s in sq)
 
         def norm(t, _):
@@ -291,7 +308,7 @@
                     on_ref[hh, :, sixteen(t), i2 * 128:(i2 + 1) * 128] = on[:, i2, :, hh * 128:(hh + 1) * 128]
             return 0
 
-        lax.fori_loop(0, NT, norm, 0)
+        lax.fori_loop(0, NT, norm, 0, unroll=2)
 
         for kh in range(2):
             def rows(ip, _):
@@ -301,7 +318,7 @@
                 out_ref[kh, ip] = (out_ref[kh, ip].astype(F32) + g * u.astype(F32)).astype(BF16)
                 return 0
 
-            lax.fori_loop(0, 8, rows, 0)
+            lax.fori_loop(0, 8, rows, 0, unroll=8)
 
     prepare(0)
     m = maskin_ref[...].astype(F32)
@@ -309,7 +326,8 @@
         half = jnp.concatenate([m[:, zz * 64 + kh * 32:zz * 64 + kh * 32 + 32] for zz in range(NZ)], axis=1)
         for i in range(16):
             mask_ref[kh, i // 2, :, i % 2 * 128:(i % 2 + 1) * 128] = half[i:i + 1, :]
-    g_pass(0)
+    g_pass_z(0)
+    g_pass_y(0)
     g_finish(0)
     for l in range(NL):
         for kh in range(2):
@@ -325,6 +343,9 @@
             forward(l, 0, g)
 
         if l == 0:
+            g_fwd(1, 0, 0).start()
+            g_fwd(1, 0, 1).start()
+            g_pass_z(1)
             prepare(1)
 
         @pl.loop(0, NG)
@@ -334,7 +355,8 @@
             forward(l, 1, g)
 
         if l == 0:
-            g_start(1)
+            g_pass_y(1)
+            g_finish(1)
 
         @pl.loop(0, NG)
         def _(g):
@@ -346,12 +368,8 @@
             def _(k):
                 multiply(l, g * TG + k)
 
-        if l == 0:
-            g_pass(1)
         drain(l)
         finish(l)
-        if l == 0:
-            g_finish(1)
 
 
 def solution(mesh):

time: 215 us -> 200 us (0.930)
  Pallas kernels: 201 us -> 186 us
    pallas_call x1, Pallas kernels: 201 us -> 186 us  [device_fn(): call(zt, mask, al, b, opm_w_out, tri_w_ab.reshape(2, 128, 512), tri_w_gat...]
where the time goes in v3:
time: 200 us
  Pallas kernels  186 us (93%)
  local copies, waits for them, and re-layouts  8.75 us (4%)
  other arithmetic  3.97 us (2%)
    pallas_call x1, Pallas kernels, device_fn(): call(zt, mask, al, b, opm_w_out, tri_w_ab.reshape(2, 128, 512), tri_w_gat...  186 us

profile of v3, /device:TPU:0, one launch (start us, length us, event | category | flops | bytes accessed | tf_op | source)
XLA Modules:
  0.0 199.7 jit_solution(14333634935893748225)
XLA Ops:
  0.0 0.0 copy-start
  0.0 0.0 copy-start.2
  0.0 0.8 fusion.21
  0.8 0.8 fusion.20
  1.5 1.3 convert_reduce_fusion
  2.8 1.4 fusion.6
  4.2 0.0 copy-done.2
  4.3 0.0 copy-start.3
  4.3 0.8 reshape.46.wab_ref
  5.1 0.0 copy-done
  5.1 0.3 fusion.2
  5.4 0.0 copy-done.3
  5.4 0.4 fusion.4
  5.8 0.4 fusion.5
  6.3 0.5 copy.32
  6.7 0.6 copy.34
  7.3 0.0 copy-start.1
  7.3 0.2 copy.35
  7.6 0.8 reshape.45.bown_ref
  8.4 1.0 fusion.15.al_ref
  9.3 0.0 copy-done.1
  9.3 0.1 copy.30
  9.5 1.5 copy.36.zt_ref
  11.0 186.0 %layers.1 = bf16[2,8,128,256]{3,2,1,0:T(8,128)(2,1)} custom-call(bf16[2,8,128,256]{3,2,1,0:T(8,128)(2,1)} %copy.36.zt_ref, s32[16,256]{1,0:T(8,128)} %maskin_ref.1, bf16[2,1024,128]{2,1,0:T(8,128)(2,1)} %fusion.15.al_ref, bf16[2,16,16,128]{3,2,1,0:T(8,128)(2,1)} %reshape.45.bown_ref, bf16[2,1024,128]{2,1,0:T(8,128)(2,1)} %wq_ref.1, ...), custom_call_target="tpu_custom_call" | custom-call | tf_op jit(solution)/shard_map/layers/pallas_call | solution.py:427
  196.9 1.6 copy.37
  198.5 1.1 copy.38
  (3 shorter events, 0.0 us)
Async XLA Ops:
  0.0 5.1 %copy-start = (bf16[64,16,256]{2,1,0:T(8,128)(2,1)S(1)}, bf16[64,16,256]{2,1,0:T(8,128)(2,1)}, u32[]{:S(2)}) copy-start(bf16[64,16,256]{2,1,0:T(8,128)(2,1)} %param.18) | copy-start | bytes 1572868
  0.0 4.2 %copy-start.2 = (bf16[2,128,4,128]{3,2,1,0:T(4,128)(2,1)S(1)}, bf16[2,128,4,128]{3,2,1,0:T(4,128)(2,1)}, u32[]{:S(2)}) copy-start(bf16[2,128,4,128]{3,2,1,0:T(4,128)(2,1)} %param.25) | copy-start | bytes 786436
  4.3 1.2 copy-start.3
  7.3 2.0 copy-start.1

commit v4 on v3

--- a/solution.py
+++ b/solution.py
@@ -123,17 +123,20 @@
     def can_recv(up, h):
         return z - h - 1 >= 0 if up else z + h + 1 < NZ
 
-    def arrive(l, h, g, kh):
+    def on_side(up, side):
+        return (z >= 2) if (up == (side == 0)) else (z < 2)
+
+    def arrive(l, h, g, kh, side):
         for up in (False, True):
-            @pl.when(can_recv(up, h))
+            @pl.when(can_recv(up, h) & on_side(up, side))
             def _():
                 zs = z - h - 1 if up else z + h + 1
                 cp_z(l, up, h, g, kh, zs, cpart).wait_recv()
                 cp_d(l, zs, g, kh, c).start()
 
-    def forward(l, h, g):
+    def forward(l, h, g, side):
         for up in (False, True):
-            @pl.when(can_send(up, h + 1))
+            @pl.when(can_send(up, h + 1) & on_side(up, side))
             def _():
                 for kh in range(2):
                     send_z(l, up, h + 1, g, kh).start()
@@ -259,7 +262,7 @@
     def drain(l):
         @pl.loop(0, NT)
         def _(t):
-            cp_o(l, t).wait()
+            cp_o(l, t).wait_send()
 
         @pl.loop(0, NG)
         def _(g):
@@ -333,26 +336,27 @@
         for kh in range(2):
             outer(l, kh)
             project(l, kh)
-        @pl.loop(0, NG)
-        def _(g):
-            arrive(l, 0, g, 0)
-
-        @pl.loop(0, NG)
-        def _(g):
-            arrive(l, 0, g, 1)
-            forward(l, 0, g)
-
-        if l == 0:
-            g_fwd(1, 0, 0).start()
-            g_fwd(1, 0, 1).start()
-            g_pass_z(1)
-            prepare(1)
+        for side in range(2):
+            @pl.loop(0, NG)
+            def _(g):
+                arrive(l, 0, g, 0, side)
+
+            @pl.loop(0, NG)
+            def _(g):
+                arrive(l, 0, g, 1, side)
+                forward(l, 0, g, side)
+
+            if l == 0 and side == 0:
+                g_fwd(1, 0, 0).start()
+                g_fwd(1, 0, 1).start()
+                g_pass_z(1)
+                prepare(1)
 
         @pl.loop(0, NG)
         def _(g):
             for kh in range(2):
-                arrive(l, 1, g, kh)
-            forward(l, 1, g)
+                arrive(l, 1, g, kh, 0)
+            forward(l, 1, g, 0)
 
         if l == 0:
             g_pass_y(1)
@@ -361,15 +365,21 @@
         @pl.loop(0, NG)
         def _(g):
             for kh in range(2):
-                arrive(l, 2, g, kh)
+                arrive(l, 2, g, kh, 0)
             ready(l, g)
 
             @pl.loop(0, TG)
             def _(k):
                 multiply(l, g * TG + k)
 
+        @pl.loop(0, NT)
+        def _(t):
+            cp_o(l, t).wait_recv()
+
+        finish(l)
+
+    for l in range(NL):
         drain(l)
-        finish(l)
 
 
 def solution(mesh):

time: 200 us -> 207 us (1.035)
  Pallas kernels: 186 us -> 193 us
    pallas_call x1, Pallas kernels: 186 us -> 193 us  [device_fn(): call(zt, mask, al, b, opm_w_out, tri_w_ab.reshape(2, 128, 512), tri_w_gat...]
where the time goes in v4:
time: 207 us; the launch traced here: 206 us
  Pallas kernels  193 us (93%)
  local copies, waits for them, and re-layouts  8.75 us (4%)
  other arithmetic  3.97 us (2%)
    pallas_call x1, Pallas kernels, device_fn(): call(zt, mask, al, b, opm_w_out, tri_w_ab.reshape(2, 128, 512), tri_w_gat...  193 us

profile of v4, /device:TPU:0, one launch (start us, length us, event | category | flops | bytes accessed | tf_op | source)
XLA Modules:
  0.0 206.3 jit_solution(3030525641530048924)
XLA Ops:
  0.0 0.0 copy-start
  0.0 0.0 copy-start.2
  0.0 0.8 fusion.21
  0.8 0.8 fusion.20
  1.5 1.3 convert_reduce_fusion
  2.8 1.4 fusion.6
  4.2 0.0 copy-done.2
  4.3 0.0 copy-start.3
  4.3 0.8 reshape.46.wab_ref
  5.1 0.0 copy-done
  5.1 0.3 fusion.2
  5.4 0.0 copy-done.3
  5.4 0.4 fusion.4
  5.8 0.4 fusion.5
  6.3 0.5 copy.32
  6.7 0.6 copy.34
  7.3 0.0 copy-start.1
  7.3 0.2 copy.35
  7.6 0.8 reshape.45.bown_ref
  8.4 1.0 fusion.15.al_ref
  9.3 0.0 copy-done.1
  9.3 0.1 copy.30
  9.5 1.5 copy.36.zt_ref
  11.0 192.6 %layers.1 = bf16[2,8,128,256]{3,2,1,0:T(8,128)(2,1)} custom-call(bf16[2,8,128,256]{3,2,1,0:T(8,128)(2,1)} %copy.36.zt_ref, s32[16,256]{1,0:T(8,128)} %maskin_ref.1, bf16[2,1024,128]{2,1,0:T(8,128)(2,1)} %fusion.15.al_ref, bf16[2,16,16,128]{3,2,1,0:T(8,128)(2,1)} %reshape.45.bown_ref, bf16[2,1024,128]{2,1,0:T(8,128)(2,1)} %wq_ref.1, ...), custom_call_target="tpu_custom_call" | custom-call | tf_op jit(solution)/shard_map/layers/pallas_call | solution.py:437
  203.5 1.6 copy.37
  205.2 1.1 copy.38
  (3 shorter events, 0.0 us)
Async XLA Ops:
  0.0 5.1 %copy-start = (bf16[64,16,256]{2,1,0:T(8,128)(2,1)S(1)}, bf16[64,16,256]{2,1,0:T(8,128)(2,1)}, u32[]{:S(2)}) copy-start(bf16[64,16,256]{2,1,0:T(8,128)(2,1)} %param.18) | copy-start | bytes 1572868
  0.0 4.2 %copy-start.2 = (bf16[2,128,4,128]{3,2,1,0:T(4,128)(2,1)S(1)}, bf16[2,128,4,128]{3,2,1,0:T(4,128)(2,1)}, u32[]{:S(2)}) copy-start(bf16[2,128,4,128]{3,2,1,0:T(4,128)(2,1)} %param.25) | copy-start | bytes 786436
  4.3 1.2 copy-start.3
  7.3 2.0 copy-start.1

commit v5 on v3

--- a/solution.py
+++ b/solution.py
@@ -9,6 +9,8 @@
 MESH = pl.DeviceIdType.MESH
 F32, BF16 = jnp.float32, jnp.bfloat16
 NL = 2
+W = 128
+W2 = 2 * W
 NT = 8
 CC = 16
 TG = 1
@@ -31,10 +33,10 @@
     return pl.ds(pl.multiple_of(i * 16, 16), 16)
 
 
-def kernel(zt_ref, maskin_ref, al_ref, bown_ref, wq_ref, wab_ref, wg_ref, wo_ref,
+def kernel(pair_ref, maskin_ref, msa_ref, win_ref, onorm_ref, obin_ref, wq_ref, wab_ref, wg_ref, wo_ref,
            bq_ref, ni_ref, bo_ref, bgate_ref, bab_ref, nout_ref,
            out_ref,
-           cols_ref, no_ref, mask_ref, bg_ref, q_ref, wqt_ref, wabt_ref, wgt_ref, wot_ref, zn_ref, st_ref, aown_ref, arecv_ref, b_ref,
+           z_ref, al_ref, bown_ref, bst_ref, wt_ref, cols_ref, no_ref, mask_ref, bg_ref, q_ref, wqt_ref, wabt_ref, wgt_ref, wot_ref, zn_ref, st_ref, aown_ref, arecv_ref, b_ref,
            obuf_ref, osend_ref, ost_ref, on_ref,
            sgi, rgi, sgd, rgd, sown, sa, ra, sz, rz, sd, rd, so, ro):
     z, y, c = place()
@@ -46,6 +48,42 @@
         pl.semaphore_signal(bar, inc=1, device_id={'dap': dap_of(lax.rem(z + r, NZ), y, c)}, device_id_type=MESH)
     pl.semaphore_signal(bar, inc=1, device_id={'dap': ypart}, device_id_type=MESH)
     pl.semaphore_signal(bar, inc=1, device_id={'dap': cpart}, device_id_type=MESH)
+
+    def turn(w):
+        return w.astype(F32).T.astype(BF16)
+
+    low = lax.broadcasted_iota(jnp.int32, (32, W), 1) < 64
+    nul = jnp.zeros((32, W), F32)
+    bcol = []
+    for l in range(NL):
+        wt_ref[l] = turn(win_ref[l])
+        row = jnp.concatenate([obin_ref[l, 0:1, :].astype(F32), obin_ref[l, 1:2, :].astype(F32),
+                               jnp.zeros((1, 64), F32)], axis=1)
+        bcol.append(jnp.broadcast_to(row, (W, W)).T[0:64])
+
+    def msa_row(i, _):
+        x = msa_ref[i].astype(F32)
+        xc = x - jnp.mean(x, axis=1, keepdims=True)
+        var = jnp.mean(xc * xc, axis=1, keepdims=True)
+        xh = xc * lax.rsqrt(var + EPS)
+        for l in range(NL):
+            mn = (xh * onorm_ref[l, 0:1, :].astype(F32) + onorm_ref[l, 1:2, :].astype(F32)).astype(BF16)
+            ab = lax.dot_general(wt_ref[l], jnp.concatenate([mn, mn], axis=0), NTD, preferred_element_type=F32) + bcol[l]
+            a = ab[0:32]
+            al_ref[l, pl.ds(pl.multiple_of(i * 32, 32), 32), :] = jnp.where(low, a, nul).astype(BF16)
+            al_ref[l, pl.ds(pl.multiple_of(512 + i * 32, 32), 32), :] = jnp.where(low, nul, a).astype(BF16)
+            bst_ref[l, pl.ds(pl.multiple_of(i * 32, 32), 32), :] = ab[32:64].astype(BF16)
+        return 0
+
+    lax.fori_loop(0, 16, msa_row, 0, unroll=4)
+    r_b = lax.broadcasted_iota(jnp.int32, (W2, 512), 0)
+    k_b = lax.broadcasted_iota(jnp.int32, (W2, 512), 1)
+    low_b = lax.broadcasted_iota(jnp.int32, (W2, W), 1) < 64
+    sel_b = [((k_b // 32 == r_b % 16) & (k_b % 32 == r_b // 16 * 2 + par)).astype(F32).astype(BF16) for par in range(2)]
+    for l in range(NL):
+        v = [jnp.dot(sel_b[par], bst_ref[l], preferred_element_type=F32) for par in range(2)]
+        bown_ref[l] = jnp.where(low_b, v[0], v[1]).astype(BF16).reshape(16, 16, W)
+
     pl.semaphore_wait(bar, NZ + 1)
 
     def bslot(l, zz, yy, core):
@@ -148,55 +186,50 @@
     g_fwd(0, 0, 1).start()
     g_start(1)
 
-    r_i = lax.broadcasted_iota(jnp.int32, (256, 256), 0)
-    c_i = lax.broadcasted_iota(jnp.int32, (256, 256), 1)
+    r_i = lax.broadcasted_iota(jnp.int32, (W2, W2), 0)
+    c_i = lax.broadcasted_iota(jnp.int32, (W2, W2), 1)
     perm = ((r_i // 16 == c_i % 16) & (r_i % 16 == c_i // 16)).astype(F32).astype(BF16)
-
-    def turn(w):
-        return w.astype(F32).T.astype(BF16)
 
     def prepare(l):
         rows = [bq_ref[l:l + 1, :], ni_ref[l, 0:1, :], ni_ref[l, 1:2, :], bo_ref[l:l + 1, :], bgate_ref[l:l + 1, :]]
         rows = rows + [bab_ref[l, qq:qq + 1, :] for qq in range(4)]
-        rows = [v.astype(F32) for v in rows] + [jnp.zeros((7, 128), F32)]
+        rows = [v.astype(F32) for v in rows] + [jnp.zeros((7, W), F32)]
         cols_ref[l] = jnp.concatenate(rows, axis=0).T
         for n in range(2):
-            no_ref[l, n] = jnp.broadcast_to(nout_ref[l, n:n + 1, :].astype(F32), (128, 128)).T
+            no_ref[l, n] = jnp.broadcast_to(nout_ref[l, n:n + 1, :].astype(F32), (W, W)).T
 
         @pl.loop(0, 4)
         def _(blk):
-            r2 = lax.broadcasted_iota(jnp.int32, (256, 1024), 0)
-            k2 = lax.broadcasted_iota(jnp.int32, (256, 1024), 1)
+            r2 = lax.broadcasted_iota(jnp.int32, (W2, 1024), 0)
+            k2 = lax.broadcasted_iota(jnp.int32, (W2, 1024), 1)
             sel = ((k2 // 32 == r2 % 32) & (k2 % 32 == r2 // 32 + blk * 8)).astype(F32).astype(BF16)
             w = jnp.dot(sel, wq_ref[l], preferred_element_type=F32)
-            wqt_ref[l, :, pl.ds(pl.multiple_of(blk * 256, 256), 256)] = w.T.astype(BF16)
+            wqt_ref[l, :, pl.ds(pl.multiple_of(blk * W2, W2), W2)] = w.T.astype(BF16)
         for qq in range(4):
-            w = turn(wab_ref[l, :, qq * 128:(qq + 1) * 128])
-            wabt_ref[l, :, qq * CC:(qq + 1) * CC, :] = w.reshape(NT, CC, 128)
+            w = turn(wab_ref[l, :, qq * W:(qq + 1) * W])
+            wabt_ref[l, :, qq * CC:(qq + 1) * CC, :] = w.reshape(NT, CC, W)
         wgt_ref[l] = turn(wg_ref[l])
         wot_ref[l] = turn(wo_ref[l])
 
     def outer(l, kh):
         @pl.loop(0, 8, unroll=8)
         def _(dpp):
-            half = pl.ds(kh * 128, 128)
+            half = pl.ds(kh * W, W)
             bt = jnp.concatenate([bg_ref[l, dpp * 2, half, :], bg_ref[l, dpp * 2 + 1, half, :]], axis=0)
             for par in range(2):
                 for h in range(2):
-                    rows = lax.dot_general(al_ref[l, pl.ds(par * 512 + h * 256, 256), :], bt, NTD,
+                    rows = lax.dot_general(al_ref[l, pl.ds(par * 512 + h * W2, W2), :], bt, NTD,
                                            preferred_element_type=F32)
-                    rows = (rows * (1.0 / 64)).astype(BF16).reshape(4, 2, 32, 256)
+                    rows = (rows * (1.0 / 64)).astype(BF16).reshape(4, 2, 32, W2)
                     for e in range(2):
                         at = pl.ds(pl.multiple_of((dpp * 4 + e * 2 + par) * 32, 32), 32)
                         for i2 in range(2):
-                            q_ref[pl.ds(h * 4, 4), at, i2 * 128:(i2 + 1) * 128] = rows[:, i2, :, e * 128:(e + 1) * 128]
-
-        src = zt_ref if l == 0 else out_ref
+                            q_ref[pl.ds(h * 4, 4), at, i2 * W:(i2 + 1) * W] = rows[:, i2, :, e * W:(e + 1) * W]
 
         def rows(ip, _):
             upd = jnp.dot(wqt_ref[l], q_ref[ip], preferred_element_type=F32) + cols_ref[l, :, 0:1]
-            zi = (src[kh, ip].astype(F32) + upd.astype(BF16).astype(F32)).astype(BF16)
-            out_ref[kh, ip] = zi
+            zi = (z_ref[kh, ip].astype(F32) + upd.astype(BF16).astype(F32)).astype(BF16)
+            z_ref[kh, ip] = zi
             x = zi.astype(F32)
             xc = x - jnp.mean(x, axis=0, keepdims=True)
             var = jnp.mean(xc * xc, axis=0, keepdims=True)
@@ -207,7 +240,7 @@
 
     def project(l, kh):
         def chunk(t, _):
-            bias = jnp.concatenate([jnp.broadcast_to(cols_ref[l, sixteen(t), 5 + qq:6 + qq], (CC, 256))
+            bias = jnp.concatenate([jnp.broadcast_to(cols_ref[l, sixteen(t), 5 + qq:6 + qq], (CC, W2))
                                     for qq in range(4)], axis=0)
             w = wabt_ref[l, t]
 
@@ -217,15 +250,15 @@
                 at = (m * jax.nn.sigmoid(p[16:32]) * p[0:16]).astype(BF16)
                 bt = (m * jax.nn.sigmoid(p[48:64]) * p[32:48]).astype(BF16)
                 for i2 in range(2):
-                    ln = slice(i2 * 128, (i2 + 1) * 128)
-                    st_ref[sixteen(ip * 2 + i2), 0:128] = at[:, ln]
-                    st_ref[sixteen(ip * 2 + i2), 128:256] = bt[:, ln]
+                    ln = slice(i2 * W, (i2 + 1) * W)
+                    st_ref[sixteen(ip * 2 + i2), 0:W] = at[:, ln]
+                    st_ref[sixteen(ip * 2 + i2), W:W2] = bt[:, ln]
                 return 0
 
             lax.fori_loop(0, 8, rows, 0, unroll=8)
             ab = jnp.dot(perm, st_ref[...], preferred_element_type=F32).astype(BF16)
-            aown_ref[l, kh, t] = ab[:, 0:128]
-            b_ref[l, z, c, kh, t] = ab[:, 128:256]
+            aown_ref[l, kh, t] = ab[:, 0:W]
+            b_ref[l, z, c, kh, t] = ab[:, W:W2]
             return 0
 
         @pl.loop(0, NG)
@@ -277,7 +310,7 @@
         def load(t, cc, hh):
             return obuf_ref[l, hh, t, pl.ds(cc * 16, 16), :]
 
-        zero = jnp.zeros((16, 128), F32)
+        zero = jnp.zeros((16, W), F32)
 
         def add1(t, s):
             for cc in range(CC):
@@ -285,7 +318,7 @@
             return s
 
         tot = lax.fori_loop(0, NT, add1, (zero, zero), unroll=2)
-        mean = tuple(s * (1.0 / 128) for s in tot)
+        mean = tuple(s * (1.0 / W) for s in tot)
 
         def add2(t, s):
             for cc in range(CC):
@@ -294,18 +327,18 @@
             return s
 
         sq = lax.fori_loop(0, NT, add2, (zero, zero), unroll=2)
-        inv = tuple(lax.rsqrt(s * (1.0 / 128) + EPS) for s in sq)
+        inv = tuple(lax.rsqrt(s * (1.0 / W) + EPS) for s in sq)
 
         def norm(t, _):
             for cc in range(CC):
                 for hh in range(2):
                     one = pl.ds(t * CC + cc, 1)
                     v = (load(t, cc, hh) - mean[hh]) * inv[hh] * no_ref[l, 0, one, :] + no_ref[l, 1, one, :]
-                    ost_ref[pl.ds(cc * 16, 16), pl.ds(hh * 128, 128)] = v.astype(BF16)
-            on = jnp.dot(perm, ost_ref[...], preferred_element_type=F32).astype(BF16).reshape(8, 2, CC, 256)
+                    ost_ref[pl.ds(cc * 16, 16), pl.ds(hh * W, W)] = v.astype(BF16)
+            on = jnp.dot(perm, ost_ref[...], preferred_element_type=F32).astype(BF16).reshape(8, 2, CC, W2)
             for hh in range(2):
                 for i2 in range(2):
-                    on_ref[hh, :, sixteen(t), i2 * 128:(i2 + 1) * 128] = on[:, i2, :, hh * 128:(hh + 1) * 128]
+                    on_ref[hh, :, sixteen(t), i2 * W:(i2 + 1) * W] = on[:, i2, :, hh * W:(hh + 1) * W]
             return 0
 
         lax.fori_loop(0, NT, norm, 0, unroll=2)
@@ -315,7 +348,14 @@
                 u = (jnp.dot(wot_ref[l], on_ref[kh, ip], preferred_element_type=F32) + cols_ref[l, :, 3:4]).astype(BF16)
                 g = jax.nn.sigmoid(jnp.dot(wgt_ref[l], zn_ref[kh, ip], preferred_element_type=F32)
                                    + cols_ref[l, :, 4:5])
-                out_ref[kh, ip] = (out_ref[kh, ip].astype(F32) + g * u.astype(F32)).astype(BF16)
+                zi = z_ref[kh, ip].astype(F32) + g * u.astype(F32)
+                if l < NL - 1:
+                    z_ref[kh, ip] = zi.astype(BF16)
+                else:
+                    zo = zi.T.astype(BF16)
+                    for i2 in range(2):
+                        for zz in range(NZ):
+                            out_ref[ip * 2 + i2, pl.ds(zz * 64 + kh * 32, 32), :] = zo[i2 * W + zz * 32:i2 * W + zz * 32 + 32]
                 return 0
 
             lax.fori_loop(0, 8, rows, 0, unroll=8)
@@ -325,14 +365,29 @@
     for kh in range(2):
         half = jnp.concatenate([m[:, zz * 64 + kh * 32:zz * 64 + kh * 32 + 32] for zz in range(NZ)], axis=1)
         for i in range(16):
-            mask_ref[kh, i // 2, :, i % 2 * 128:(i % 2 + 1) * 128] = half[i:i + 1, :]
+            mask_ref[kh, i // 2, :, i % 2 * W:(i % 2 + 1) * W] = half[i:i + 1, :]
+
+    def bring(ip, _):
+        for kh in range(2):
+            for i2 in range(2):
+                rows = jnp.concatenate([pair_ref[ip * 2 + i2, pl.ds(zz * 64 + kh * 32, 32), :] for zz in range(NZ)], axis=0)
+                z_ref[kh, ip, :, i2 * W:(i2 + 1) * W] = turn(rows)
+        return 0
+
     g_pass_z(0)
+    lax.fori_loop(0, 8, bring, 0, unroll=2)
     g_pass_y(0)
     g_finish(0)
     for l in range(NL):
         for kh in range(2):
             outer(l, kh)
             project(l, kh)
+            if l == 0 and kh == 0:
+                g_fwd(1, 0, 0).start()
+                g_fwd(1, 0, 1).start()
+                g_pass_z(1)
+        if l == 0:
+            prepare(1)
         @pl.loop(0, NG)
         def _(g):
             arrive(l, 0, g, 0)
@@ -341,12 +396,6 @@
         def _(g):
             arrive(l, 0, g, 1)
             forward(l, 0, g)
-
-        if l == 0:
-            g_fwd(1, 0, 0).start()
-            g_fwd(1, 0, 1).start()
-            g_pass_z(1)
-            prepare(1)
 
         @pl.loop(0, NG)
         def _(g):
@@ -356,7 +405,6 @@
 
         if l == 0:
             g_pass_y(1)
-            g_finish(1)
 
         @pl.loop(0, NG)
         def _(g):
@@ -370,6 +418,8 @@
 
         drain(l)
         finish(l)
+        if l == 0:
+            g_finish(1)
 
 
 def solution(mesh):
@@ -387,16 +437,17 @@
 
     call = pl.pallas_call(
         kernel,
-        out_shape=jax.ShapeDtypeStruct((2, 8, 128, 256), BF16),
-        in_specs=[vm] * 14,
+        out_shape=jax.ShapeDtypeStruct((16, W2, W), BF16),
+        in_specs=[vm] * 16,
         out_specs=vm,
         scratch_shapes=[
-            f3(NL, 128, 16), f3(NL, 2, 128, 128), f3(2, 8, 1, 256),
-            bf(NL, 16, 256, 128), bf(8, 1024, 256),
-            bf(NL, 128, 1024), bf(NL, NT, 4 * CC, 128), bf(NL, 128, 128), bf(NL, 128, 128),
-            bf(2, 8, 128, 256), bf(256, 256),
-            bf(NL, 2, NT, 256, 128), bf(NL, 2, NT, 256, 128), bf(NL, NZ, 2, 2, NT, 256, 128),
-            f3(NL, 2, NT, 256, 128), f3(NL, NT, 256, 128), bf(256, 256), bf(2, 8, 128, 256),
+            bf(2, 8, W, W2), bf(NL, 1024, W), bf(NL, 16, 16, W), bf(NL, 512, W), bf(NL, 64, W2),
+            f3(NL, W, 16), f3(NL, 2, W, W), f3(2, 8, 1, W2),
+            bf(NL, 16, W2, W), bf(8, 1024, W2),
+            bf(NL, W, 1024), bf(NL, NT, 4 * CC, W), bf(NL, W, W), bf(NL, W, W),
+            bf(2, 8, W, W2), bf(W2, W2),
+            bf(NL, 2, NT, W2, W), bf(NL, 2, NT, W2, W), bf(NL, NZ, 2, 2, NT, W2, W),
+            f3(NL, 2, NT, W2, W), f3(NL, NT, W2, W), bf(W2, W2), bf(2, 8, W, W2),
             dma((NL, 8)), dma((NL, 8)), dma((NL, 8)), dma((NL, 8)), dma((NL,)),
             dma((NL, NG, 2)), dma((NL, NG, 2)),
             dma((NL, 2, NZ - 1, NG, 2)), dma((NL, 2, NZ - 1, NG, 2)),
@@ -409,24 +460,9 @@
 
     def device_fn(pair, mask, msa, opm_norm, opm_w_in, opm_b_in, opm_w_out, opm_b_out, tri_norm_in, tri_w_ab, tri_b_ab,
                   tri_w_gate, tri_b_gate, tri_norm_out, tri_w_out, tri_b_out):
-        x = msa.astype(F32)
-        xc = x - jnp.mean(x, axis=-1, keepdims=True)
-        var = jnp.mean(xc * xc, axis=-1, keepdims=True)
-        xh = xc * lax.rsqrt(var + EPS)
-        nw = opm_norm.astype(F32)
-        mn = (xh[None] * nw[:, 0][:, None, None] + nw[:, 1][:, None, None]).astype(BF16)
-        bias = opm_b_in.astype(F32)
-        b = (jnp.einsum('lmd,lsjm->ldjs', opm_w_in[:, :, 1], mn, preferred_element_type=F32)
-             + bias[:, 1][:, :, None, None]).astype(BF16)
-        b = b.reshape(2, 16, 2, 16, 64).transpose(0, 1, 3, 2, 4).reshape(2, 16, 16, 128)
-        a = (jnp.einsum('lmc,lsim->lics', opm_w_in[:, :, 0], mn, preferred_element_type=F32)
-             + bias[:, 0][:, None, :, None]).astype(BF16).reshape(2, 512, 64)
-        al = jnp.concatenate([jnp.pad(a, ((0, 0), (0, 0), (0, 64))), jnp.pad(a, ((0, 0), (0, 0), (64, 0)))], axis=1)
-
-        zt = pair.reshape(8, 2, 4, 2, 32, 128).transpose(3, 0, 5, 1, 2, 4).reshape(2, 8, 128, 256)
-        zt = call(zt, mask, al, b, opm_w_out, tri_w_ab.reshape(2, 128, 512), tri_w_gate, tri_w_out,
-                  opm_b_out, tri_norm_in, tri_b_out, tri_b_gate, tri_b_ab, tri_norm_out)
-        return zt.reshape(2, 8, 128, 2, 4, 32).transpose(1, 3, 4, 0, 5, 2).reshape(16, 256, 128)
+        return call(pair, mask, msa.transpose(1, 0, 2), opm_w_in.reshape(2, W2, 64), opm_norm, opm_b_in,
+                    opm_w_out, tri_w_ab.reshape(2, W, 512), tri_w_gate, tri_w_out,
+                    opm_b_out, tri_norm_in, tri_b_out, tri_b_gate, tri_b_ab, tri_norm_out)
 
     return jax.shard_map(device_fn, mesh=mesh, in_specs=(pair_spec, mask_spec, msa_spec) + (P(),) * 13,
                          out_specs=pair_spec, check_vma=False)

time: 200 us -> 193 us (0.965)
  other arithmetic: 3.97 us -> 0 us
  local copies, waits for them, and re-layouts: 8.75 us -> 6.67 us
    unnamed x9 -> x4, local copies, waits for them, and re-layouts: 0.03 us -> 3.25 us
    reduce_sum x2 -> x0, other arithmetic: 2.65 us -> none  [the longest x1 1.4 us: device_fn(): var = jnp.mean(xc * xc, axis=-1, keepdims=True)]
where the time goes in v5:
time: 193 us
  Pallas kernels  186 us (96%)
  local copies, waits for them, and re-layouts  6.67 us (3%)
    pallas_call x1, Pallas kernels, device_fn(): call(pair, mask, msa.transpose(1, 0, 2), opm_w_in.reshape(2, W2, 64), opm...  186 us

profile of v5, /device:TPU:0, one launch (start us, length us, event | category | flops | bytes accessed | tf_op | source)
XLA Modules:
  0.0 193.0 jit_solution(9144994083894857839)
XLA Ops:
  0.0 0.0 copy-start
  0.0 1.7 copy.20.win_ref
  1.7 1.8 reshape.7.wab_ref
  3.4 0.0 copy-done
  3.4 1.0 copy.22
  4.4 186.3 %layers.1 = bf16[16,256,128]{2,1,0:T(8,128)(2,1)} custom-call(bf16[16,256,128]{2,1,0:T(8,128)(2,1)} %pair_ref.1, s32[16,256]{1,0:T(8,128)} %maskin_ref.1, bf16[16,64,256]{2,1,0:T(8,128)(2,1)} %bitcast.4, bf16[2,256,64]{2,1,0:T(8,128)(2,1)} %copy.20.win_ref, bf16[2,2,256]{2,1,0:T(2,128)(2,1)} %onorm_ref.1, bf16[2,2,32]{2,1,0:T(2,128)(2,1)} %obin_ref.1, ...), custom_call_target="tpu_custom_call" | custom-call | tf_op jit(solution)/shard_map/layers/pallas_call | solution.py:463
  190.7 2.3 %copy.24 = bf16[16,256,128]{2,1,0:T(8,128)(2,1)} copy(bf16[16,256,128]{2,1,0:T(8,128)(2,1)} %layers.1) | data formatting | bytes 2097152
Async XLA Ops:
  0.0 3.4 %copy-start = (bf16[64,16,256]{2,1,0:T(8,128)(2,1)S(1)}, bf16[64,16,256]{2,1,0:T(8,128)(2,1)}, u32[]{:S(2)}) copy-start(bf16[64,16,256]{2,1,0:T(8,128)(2,1)} %param.18) | copy-start | bytes 1572868
